TPU v7x, 128 devices: a whole 4x4x4 slice. The times are simulated.
128 devices in a mesh: blk: 64 (over z_lo, x, y, core), slab: 2 (over z_hi).
Axes of the slice: x: 4, y: 4, z: 4 (z_hi: 2, z_lo: 2; z = z_hi * 2 + z_lo), core: 2. Of those that a mesh axis runs over, the one named last changes fastest.
Arguments:
- sinogram: bfloat16 [128, 8, 2048], P('blk', 'slab'), parts along dimension 1, may hold values from -6 to 6
- jitter: bfloat16 [128], P('blk'), may hold values from -0.29882812 to 0.29882812
- shift: int32 [128], replicated, may hold values from -8 to 8
Outputs:
- image: float32 [128, 8, 2048], P('blk', 'slab'), parts along dimension 1
There are 2 independent parts, one for each index of `slab`. A program takes and returns all parts, laid end to end along the dimension named above; an argument that names none is the same for every part. Nothing has to cross between parts.
All inputs are finite; a program needn't handle non-finite values.
Results may differ from a plain program's by a relative error of at most 0.0055.
Values may be sent and summed in bfloat16 or wider, within the bound.
A program may use at most 64 MiB of HBM per device.

v0:
```python
import math

import jax
import jax.numpy as jnp
from jax import lax
from jax.sharding import Mesh
from jax.sharding import PartitionSpec as P

ROWS_DEV = 2
BLK = ("blk_0", "blk_1", "blk_2", "blk_3")


def padded(cells, sides, width):
    for axis, dim in sides:
        count = lax.axis_size(axis)
        head = lax.slice_in_dim(cells, 0, width, axis=dim)
        tail = lax.slice_in_dim(cells, cells.shape[dim] - width, cells.shape[dim], axis=dim)
        cells = jnp.concatenate(
            [
                lax.ppermute(tail, axis, [(i, (i + 1) % count) for i in range(count)]),
                cells,
                lax.ppermute(head, axis, [((i + 1) % count, i) for i in range(count)]),
            ],
            axis=dim,
        )
    return cells


def split_up(x, dim, devices):
    lengths = x.shape
    pieces = x.reshape(*lengths[:dim], devices, lengths[dim] // devices, *lengths[dim + 1 :])
    return jnp.moveaxis(pieces, dim, 0)


def summed_rows(x, chips, core, dim):
    sizes = (lax.axis_size(chips), lax.axis_size(core))
    pieces = split_up(x, dim, sizes[0] * sizes[1])
    inside = pieces.shape[1:]
    pieces = pieces.reshape(*sizes, *inside).swapaxes(0, 1).reshape(-1, *inside)
    pieces = lax.psum_scatter(pieces, core, scatter_dimension=0, tiled=True)
    return lax.psum_scatter(pieces, chips, scatter_dimension=0, tiled=True)[0]


def ramp_matrix(bins):
    offsets = (
        jnp.arange(bins, dtype=jnp.int32)[None, :] - jnp.arange(bins, dtype=jnp.int32)[:, None]
    )
    safe = jnp.where(offsets == 0, 1, offsets).astype(jnp.float32)
    odd_part = jnp.where(offsets % 2 != 0, -1.0 / (math.pi**2 * safe * safe), jnp.float32(0.0))
    kernel = jnp.where(offsets == 0, jnp.float32(0.25), odd_part)
    return kernel.astype(jnp.bfloat16)


def contribute(frow, theta, offset, row_count, nrows):
    slices, bins = frow.shape
    nblocks = bins // 128
    pad_tiles = bins // 512 + 2
    tile_count = nblocks + 2 * pad_tiles
    pad_bins = pad_tiles * 128
    tiled = jnp.pad(frow, ((0, 0), (pad_bins, pad_bins))).reshape(slices, tile_count, 128)
    coords_x = (jnp.arange(bins, dtype=jnp.float32) - (bins - 1) / 2).reshape(nblocks, 128)
    row_pos = jnp.arange(row_count, dtype=jnp.int32).astype(jnp.float32) - (nrows - 1) / 2
    cosine = jnp.cos(theta)
    sine_part = jnp.sin(theta)
    center_bin = (bins - 1) / 2 + offset.astype(jnp.float32)
    coords = coords_x[None, :, :] * cosine + row_pos[:, None, None] * sine_part + center_bin
    lowest = jnp.minimum(coords[:, :, 0], coords[:, :, 127])
    first_tile = jnp.clip(
        (jnp.floor(lowest).astype(jnp.int32) + pad_bins) // 128, 0, tile_count - 3
    )
    first_tile = first_tile.reshape(row_count * nblocks)
    wanted = first_tile[:, None] + jnp.arange(3, dtype=jnp.int32)[None, :]
    selector = (
        wanted[:, :, None] == jnp.arange(tile_count, dtype=jnp.int32)[None, None, :]
    ).astype(jnp.bfloat16)
    strips = jnp.einsum(
        "njt,stk->nsjk", selector, tiled, preferred_element_type=jnp.float32
    ).astype(jnp.bfloat16)
    strips = strips.reshape(row_count * nblocks, slices, 3 * 128)
    detector = (
        first_tile[:, None] * 128 + jnp.arange(3 * 128, dtype=jnp.int32)[None, :] - pad_bins
    ).astype(jnp.float32)
    flat_coords = coords.reshape(row_count * nblocks, 128)
    weights = jnp.maximum(
        0.0, 1.0 - jnp.abs(detector[:, :, None] - flat_coords[:, None, :])
    ).astype(jnp.bfloat16)
    return jnp.einsum("nsb,nbc->nsc", strips, weights, preferred_element_type=jnp.float32)


def body(sinogram, jitter, shift):
    ang_dev, slices, bins = sinogram.shape
    width = lax.axis_size(BLK)
    angles = width * ang_dev
    nrows = ROWS_DEV * width
    nblocks = bins // 128
    here = lax.axis_index(BLK)
    extended = padded(jitter, ((BLK, 0),), 1).astype(jnp.float32)
    weight = (1.0 + (extended[2:] - extended[:-2]) * 1.5) * (4.0 / math.sqrt(angles))
    ramp = ramp_matrix(bins)
    flat = jnp.dot(
        sinogram.reshape(ang_dev * slices, bins), ramp, preferred_element_type=jnp.float32
    )
    filtered = (flat.reshape(ang_dev, slices, bins) * weight[:, None, None]).astype(jnp.bfloat16)
    first = here * ang_dev
    count = ROWS_DEV * lax.axis_size(("blk_0", "blk_1", "blk_2")) * lax.axis_size("blk_3")

    def one_angle(position, accum):
        angle_id = first + position
        deviation = lax.dynamic_index_in_dim(jitter, position, 0, False).astype(jnp.float32)
        theta = (angle_id.astype(jnp.float32) + deviation) * math.pi / angles
        offset = lax.dynamic_index_in_dim(shift, angle_id, 0, False)
        frow = lax.dynamic_index_in_dim(filtered, position, 0, False)
        return accum + contribute(frow, theta, offset, count, nrows)

    accum = lax.fori_loop(
        0, ang_dev, one_angle, jnp.zeros((count * nblocks, slices, 128), jnp.float32)
    )
    return summed_rows(
        accum.reshape(count, nblocks, slices, 128)
        .transpose(0, 2, 1, 3)
        .reshape(count, slices, bins),
        ("blk_0", "blk_1", "blk_2"),
        "blk_3",
        0,
    )


def solution(mesh):
    split = Mesh(
        mesh.devices.reshape(2, 4, 4, 2, mesh.shape["slab"]),
        ("blk_0", "blk_1", "blk_2", "blk_3", "slab"),
    )
    placed = (P(BLK, "slab", None), P(BLK), P())
    return jax.shard_map(
        body, mesh=split, in_specs=placed, out_specs=P(BLK, "slab", None), check_vma=False
    )
```

profile of v0, /device:TPU:0, one launch (start us, length us, event | category | flops | bytes accessed | tf_op | source)
XLA Modules:
  0.0 693.9 jit_solution(14447127050756065846)
XLA Ops:
  6.5 1.3 fusion.36
  7.9 0.0 collective-permute-start
  7.9 6.1 collective-permute-start.1
  14.0 0.8 reshape.204
  14.8 0.0 copy-start
  14.8 0.0 copy-start.1
  14.8 13.4 %fusion.26 = f32[8,2048]{1,0:T(8,128)S(1)} fusion(bf16[8,2048]{1,0:T(8,128)(2,1)S(1)} %reshape.204), kind=kOutput, calls=%fused_computation.50 | convolution fusion | flops 159383552 | bytes 98304 | tf_op jit(solution)/shard_map/dot_general | solution.py:100
  28.2 0.0 collective-permute-done
  28.2 0.0 collective-permute-done.1
  28.3 1.3 maximum_convert_fusion.4
  29.6 0.1 add_multiply_fusion.2
  29.7 0.1 multiply_convert_fusion
  29.8 305.7 %while.16 = (s32[]{:T(128)}, f32[2048,4,128]{2,1,0:T(4,128)}, bf16[2,4,2048]{2,1,0:T(4,128)(2,1)S(1)}, s32[]{:T(128)}, bf16[2]{0:T(256)(128)(2,1)S(1)}, /*index=...) while((s32[]{:T(128)}, f32[2048,4,128]{2,1,0:T(4,128)}, ...), condition=%wide.region_1.2_spmd.clone, body=%wide.region_0.1_spmd.clone.sunk | while | flops 1493664128 | bytes 43345688 | solution.py:115
  29.8 0.6 dynamic_slice.41
  30.9 0.6 dynamic_slice.42
  32.3 0.2 add_add_fusion.2
  32.5 2.5 fusion.48
  35.0 0.1 add.482
  35.2 4.5 convolution_convert_fusion.2
  39.7 10.7 %copy.19 = bf16[2048,4,384]{2,1,0:T(4,128)(2,1)} copy(bf16[2048,4,384]{0,2,1:T(8,128)(2,1)} %bitcast.50) | data formatting | bytes 12582912 | tf_op jit(solution)/shard_map/while/body/eval_jaxpr/reshape | solution.py:79
  50.4 0.4 add_convert_fusion.2
  50.8 0.1 add.483
  50.9 0.1 add.484
  51.0 1.3 fusion.49
  52.3 130.3 %select_add_fusion.2 = f32[2048,4,128]{2,1,0:T(4,128)} fusion(f32[2048,4,128]{2,1,0:T(4,128)} %get-tuple-element.257, bf16[2048,4,384]{2,1,0:T(4,128)(2,1)} %copy.19, f32[2048,128]{1,0:T(8,128)} %fusion.49, f32[2048,384]{1,0:T(8,128)S(1)} %add_convert_fusion.2, pred[]{:T(512)S(6)} %compare.34), kind=kOutput, calls=%fused_computation.3.clone.2 | convolution fusion | flops 1310720000 | bytes 18874368 | tf_op jit(solution)/shard_map/while/body/eval_jaxpr/nsb,nbc->nsc/dot_general | solution.py:87
  182.6 0.6 dynamic_slice.41
  183.8 0.6 dynamic_slice.42
  185.1 0.2 add_add_fusion.2
  185.3 2.5 fusion.48
  187.8 0.1 add.482
  188.0 4.5 convolution_convert_fusion.2
  192.5 10.7 %copy.19 = bf16[2048,4,384]{2,1,0:T(4,128)(2,1)} copy(bf16[2048,4,384]{0,2,1:T(8,128)(2,1)} %bitcast.50) | data formatting | bytes 12582912 | tf_op jit(solution)/shard_map/while/body/eval_jaxpr/reshape | solution.py:79
  203.3 0.4 add_convert_fusion.2
  203.6 0.1 add.483
  203.7 0.1 add.484
  203.8 1.3 fusion.49
  205.1 130.4 %select_add_fusion.2 = f32[2048,4,128]{2,1,0:T(4,128)} fusion(f32[2048,4,128]{2,1,0:T(4,128)} %get-tuple-element.257, bf16[2048,4,384]{2,1,0:T(4,128)(2,1)} %copy.19, f32[2048,128]{1,0:T(8,128)} %fusion.49, f32[2048,384]{1,0:T(8,128)S(1)} %add_convert_fusion.2, pred[]{:T(512)S(6)} %compare.34), kind=kOutput, calls=%fused_computation.3.clone.2 | convolution fusion | flops 1310720000 | bytes 18874368 | tf_op jit(solution)/shard_map/while/body/eval_jaxpr/nsb,nbc->nsc/dot_general | solution.py:87
  335.5 4.7 copy.17
  340.2 5.3 reshape_reshape_reshape.3
  345.4 6.5 copy.13
  352.0 0.0 reduce-scatter.2.cloned.1.call-update
  352.0 0.0 all-reduce.4.cloned.1.call-start
  352.0 12.9 %reduce-scatter.2.cloned.1.call-done = f32[32,2,4,2048]{3,0,2,1:T(8,128)} async-done(((f32[64,2,4,2048]{3,0,2,1:T(8,128)}), f32[32,2,4,2048]{3,0,2,1:T(8,128)}) %reduce-scatter.2.cloned.1.call-update) | async-done | bytes 2097168 | tf_op jit(solution)/shard_map/reduce_scatter | solution.py:40
  365.0 4.3 copy.14
  369.3 0.0 all-reduce.4.cloned.1.call-update
  369.3 0.6 dynamic-slice
  369.9 315.0 %all-reduce.4.cloned.1.call-done = f32[32,2,4,2048]{3,2,1,0:T(4,128)} async-done(((f32[32,2,4,2048]{3,2,1,0:T(4,128)}), f32[32,2,4,2048]{3,2,1,0:T(4,128)}) %all-reduce.4.cloned.1.call-update) | async-done | bytes 2097168
  685.0 2.1 dynamic-slice_bitcast_fusion.1
  (21 shorter events, 0.3 us)
Async XLA Ops:
  6.5 358.4 %reduce-scatter.2.cloned.1.call-start = ((), (), s32[]{:S(2)}) async-start(), calls=%async_computation.1 | async-start | bytes 6291456 | tf_op jit(solution)/shard_map/reduce_scatter | solution.py:40
  7.9 20.4 %collective-permute-start = (bf16[1]{0:T(256)(128)(2,1)}, bf16[1]{0:T(256)(128)(2,1)}, u32[]{:S(2)}, u32[]{:S(2)}) collective-permute-start(bf16[1]{0:T(256)(128)(2,1)} %get-tuple-element.201), channel_id=1, source_target_pairs={{0,2},{2,4},{4,6},{6,8},{8,10},{10,12},{12,14},{14,16},{16,18},{18... | collective-permute-start | bytes 14 | tf_op jit(solution)/shard_map/ppermute | solution.py:20
  7.9 20.4 %collective-permute-start.1 = (bf16[1]{0:T(256)(128)(2,1)}, bf16[1]{0:T(256)(128)(2,1)}, u32[]{:S(2)}, u32[]{:S(2)}) collective-permute-start(bf16[1]{0:T(256)(128)(2,1)} %get-tuple-element.202), channel_id=1, source_target_pairs={{2,0},{4,2},{6,4},{8,6},{10,8},{12,10},{14,12},{16,14},{18,16},{20... | collective-permute-start | bytes 14 | tf_op jit(solution)/shard_map/ppermute | solution.py:22
  14.8 13.5 %copy-start = (bf16[2]{0:T(256)(128)(2,1)S(1)}, bf16[2]{0:T(256)(128)(2,1)}, u32[]{:S(2)}) copy-start(bf16[2]{0:T(256)(128)(2,1)} %param.6) | copy-start | bytes 16
  14.8 15.0 %copy-start.1 = (s32[128]{0:T(128)S(1)}, s32[128]{0:T(128)}, u32[]{:S(2)}) copy-start(s32[128]{0:T(128)} %param.7) | copy-start | bytes 1540
  352.0 17.3 %copy-start.2 = (u32[128]{0:T(128)S(1)}, u32[128]{0:T(128)}, u32[]{:S(2)}) copy-start(u32[128]{0:T(128)} %constant.234) | copy-start | bytes 1540
  352.0 333.0 %all-reduce.4.cloned.1.call-start = ((), (), s32[]{:S(2)}) async-start(), calls=%async_computation.2 | async-start | bytes 4194304
Sparse Core Ops, SparseCore 0:
  352.1 12.8 reduce-scatter.1
  369.4 315.5 all-reduce.3
where the time goes:
time: 695 us; the launch traced here: 694 us
  waiting for transfers between devices  328 us (47%)
  matrix products  283 us (41%)
  local copies, waits for them, and re-layouts  50 us (7%)
  between operations  13.5 us (2%)
  other arithmetic  10.4 us (1%)
    unnamed x3, waiting for transfers between devices  315 us
    dot_general x2, matrix products, contribute(): jnp.einsum('nsb,nbc->nsc', strips, weights, preferred_element_type=jnp.fl...  261 us
    reshape x2, local copies, waits for them, and re-layouts, contribute(): strips = strips.reshape(row_count * nblocks, slices, 3 * 128)  21.5 us
  transfers between devices with their start and end apart: 4, of which 2 were waited for; matrix products, arithmetic and copies ran while one was open for 2% of the time, Pallas kernels for 0%

commit v1 on v0

v1 whole, which is shorter than its diff:
```python
import functools
import math

import jax
import jax.numpy as jnp
from jax import lax
from jax.experimental import pallas as pl
from jax.experimental.pallas import tpu as pltpu
from jax.sharding import PartitionSpec as P

BINS = 2048
ANGLES = 128
NROWS = 128
TILES = 18
STRIP = 3968
F32 = jnp.float32
BF16 = jnp.bfloat16


def hop(r):
    dz = jnp.where((r == 0) | (r == 1) | (r == 2) | (r == 6), 0, 1)
    dx = jnp.where(
        (r == 0) | (r == 3), 0, jnp.where((r == 1) | (r == 4), 1, jnp.where((r == 2) | (r == 5), 3, 2))
    )
    return dz, dx


def source_of(m, r):
    dz, dx = hop(r)
    return ((m // 4 + dz) % 2) * 4 + (m % 4 + 4 - dx) % 4


def target_of(m, r):
    dz, dx = hop(r)
    return ((m // 4 + dz) % 2) * 4 + (m % 4 + dx) % 4


def lane_gather(x, idx):
    return jnp.take_along_axis(x, idx, axis=1, mode="promise_in_bounds")


def build_strip(strip):
    shape = (128, 128)
    diff = lax.broadcasted_iota(jnp.int32, shape, 1) - lax.broadcasted_iota(jnp.int32, shape, 0)
    odd = (diff % 2) != 0
    diff_f = diff.astype(F32)

    def chunk(c, _):
        n = diff_f + (1920 - 128 * c).astype(F32)
        value = jnp.where(odd, (-1.0 / math.pi**2) / (n * n), 0.0)
        value = jnp.where(n == 0.0, 0.25, value)
        strip[pl.ds(pl.multiple_of(c * 128, 128), 128), :] = value.astype(BF16)
        return 0

    lax.fori_loop(0, STRIP // 128, chunk, 0)


def filter_rows(sino, strip, flat, msg):
    x = jnp.concatenate([sino[0].astype(F32), sino[1].astype(F32)], axis=0)
    xs = jnp.concatenate([x[:, 256 * i : 256 * i + 256] for i in range(8)], axis=0).astype(BF16)
    for d in range(-7, 8):
        rhs = jnp.concatenate(
            [strip[1920 - 128 * e : 1920 - 128 * e + 256, :] for e in (2 * d, 2 * d + 1)], axis=1
        )
        part = jnp.dot(xs, rhs, preferred_element_type=F32)
        for i in range(max(0, -d), min(8, 8 - d)):
            j = i + d
            piece = part[8 * i : 8 * i + 8, :]
            if i == 7:
                flat[8 * j : 8 * j + 8, :] = piece
            else:
                flat[8 * j : 8 * j + 8, :] += piece
    for j in range(8):
        msg[0, :, 256 * j : 256 * j + 256] = flat[8 * j : 8 * j + 8, :].astype(BF16)


def kernel(
    sino, jit, shift, out,
    strip, flat, msg, jr, fbuf, dbuf, tab, tabi, stab, stabi, acc, turn, sendb, recvb,
    jsend, jrecv, msend, mrecv, rsend, rrecv, tsem,
):
    idx = lax.axis_index("blk")
    m = idx // 8
    j = idx % 8
    barrier = pltpu.get_barrier_semaphore()

    def device(mm, jj):
        return {"blk": mm * 8 + jj}

    for dj in (-1, 0, 1):
        for r in range(8):
            if dj == 0 and r == 0:
                continue
            pl.semaphore_signal(barrier, inc=1, device_id=device(target_of(m, r), (j + dj + 8) % 8))
    for dj in (2, 3, 4, 5, 6):
        pl.semaphore_signal(barrier, inc=1, device_id=device(m, (j + dj) % 8))

    lane1 = lax.broadcasted_iota(jnp.int32, (1, 128), 1)
    second1 = ((lane1 // 32) == 1) | ((lane1 // 32) == 2)
    jv = jit[...].astype(F32)
    jrow = jnp.where(second1, jnp.broadcast_to(jv[:, 1:2], (1, 128)), jnp.broadcast_to(jv[:, 0:1], (1, 128)))
    jr[8] = jrow

    build_strip(strip)
    filter_rows(sino, strip, flat, msg)

    pl.semaphore_wait(barrier, 28)

    jcopies = []
    for dj in (-1, 0, 1):
        jj = (j - dj + 8) % 8
        base = m if dj == 0 else (jnp.where(j == 0, (m + 7) % 8, m) if dj == 1 else jnp.where(j == 7, (m + 1) % 8, m))
        for r in range(8):
            if dj == 0 and r == 0:
                continue
            slot = (dj + 1) * 8 + r
            jcopies.append(
                pltpu.make_async_remote_copy(
                    src_ref=jr.at[8], dst_ref=jr.at[slot],
                    send_sem=jsend.at[slot], recv_sem=jrecv.at[slot],
                    device_id=device(target_of(base, r), jj),
                )
            )
    for c in jcopies:
        c.start()
    mcopies = []
    for r in range(1, 8):
        mcopies.append(
            pltpu.make_async_remote_copy(
                src_ref=msg.at[0], dst_ref=msg.at[r],
                send_sem=msend.at[r], recv_sem=mrecv.at[r],
                device_id=device(target_of(m, r), j),
            )
        )
    for c in mcopies:
        c.start()

    for c in jcopies:
        c.wait_recv()
    shape = (8, 128)
    lane = lax.broadcasted_iota(jnp.int32, shape, 1)
    sub = lax.broadcasted_iota(jnp.int32, shape, 0)
    a_l = (lane // 32) % 2
    g_l = (lane // 16) % 2
    k_l = lane % 16

    def rows_of(start):
        return jnp.concatenate([jr[start + r] for r in range(8)], axis=0)

    here = rows_of(8)
    before = pltpu.roll(rows_of(0), 64, 1)
    after = pltpu.roll(rows_of(16), 64, 1)
    other = pltpu.roll(here, 64, 1)
    nxt = jnp.where(a_l == 0, other, after)
    prv = jnp.where(a_l == 1, other, before)
    weight = (1.0 + (nxt - prv) * 1.5) * (4.0 / math.sqrt(ANGLES))
    angle = source_of(m, sub) * 16 + 2 * j + a_l
    theta = (angle.astype(F32) + here) * math.pi / ANGLES
    cosine = jnp.cos(theta)
    sine = jnp.sin(theta)
    offset = lane_gather(jnp.broadcast_to(shift[...], shape), angle).astype(F32)
    center = (
        cosine * (128.0 * k_l.astype(F32) - (BINS - 1) / 2)
        + sine * ((16 * m + 8 * g_l).astype(F32) - (NROWS - 1) / 2)
        + ((BINS - 1) / 2 + 128.0 + offset)
    )
    lowest = center + jnp.minimum(0.0, 127.0 * cosine) + jnp.minimum(0.0, 7.0 * sine) - 0.01
    tile_f = jnp.floor(lowest * (1.0 / 128.0))
    tab[0] = center - 128.0 * tile_f
    tab[1] = weight
    tab[2] = cosine
    tab[3] = sine
    tabi[...] = jnp.clip(tile_f.astype(jnp.int32), 0, TILES - 2)
    tc = pltpu.make_async_copy(tab, stab, tsem.at[0])
    ti = pltpu.make_async_copy(tabi, stabi, tsem.at[1])
    tc.start()
    ti.start()
    acc[...] = jnp.zeros_like(acc)
    tc.wait()
    ti.wait()

    last = lane == 127
    lane_f = lane.astype(F32)
    sub_f = sub.astype(F32)
    zero = jnp.zeros(shape, F32)

    def one_source(r, _):
        @pl.when(r > 0)
        def _():
            pltpu.make_async_copy(msg.at[r], msg.at[r], mrecv.at[r]).wait()

        w = jnp.where(sub < 4, stab[1, r, 0], stab[1, r, 32])
        base = r * (TILES * 8)

        def put(ref, t, value):
            ref[pl.ds(pl.multiple_of(base + t * 8, 8), 8), :] = value

        prev, prev_rolled = zero, zero
        put(fbuf, 0, zero)
        for t in range(1, TILES):
            if t < TILES - 1:
                f = msg[r, :, 128 * (t - 1) : 128 * t].astype(F32) * w
                rolled = pltpu.roll(f, 127, 1)
            else:
                f, rolled = zero, zero
            put(fbuf, t, f)
            put(dbuf, t - 1, jnp.where(last, rolled, prev_rolled) - prev)
            prev, prev_rolled = f, rolled
        put(dbuf, TILES - 1, zero)

        ramps = [stab[2, r, 32 * a] * lane_f + stab[3, r, 32 * a] * sub_f for a in range(2)]

        def one_group(g, _):
            for k in range(16):
                total = [acc[g, k, s] for s in range(4)]
                for a in range(2):
                    col = 32 * a + 16 * g + k
                    v = ramps[a] + stab[0, r, col]
                    row = base + stabi[r, col] * 8 + 4 * a
                    cell = v.astype(jnp.int32)
                    frac = v - cell.astype(F32)
                    upper = cell >= 128
                    pick = cell & 127
                    for s in range(4):
                        def at(ref, shift_rows):
                            one = ref[pl.ds(row + (s + shift_rows), 1), :]
                            return lane_gather(jnp.broadcast_to(one, shape), pick)

                        f = jnp.where(upper, at(fbuf, 8), at(fbuf, 0))
                        d = jnp.where(upper, at(dbuf, 8), at(dbuf, 0))
                        total[s] = total[s] + (f + frac * d)
                for s in range(4):
                    acc[g, k, s] = total[s]
            return 0

        lax.fori_loop(0, 2, one_group, 0)
        return 0

    lax.fori_loop(0, 8, one_source, 0)

    for g in range(2):
        for k in range(16):
            for s in range(4):
                turn[g, k, pl.ds(s, 8, stride=4), :] = acc[g, k, s]
    for g in range(2):
        for q in range(4):
            for k in range(16):
                sendb[4 * g + q, :, 128 * k : 128 * k + 128] = turn[g, k, 8 * q : 8 * q + 8, :].astype(BF16)
    rcopies = []
    for dj in range(1, 8):
        jj = (j + dj) % 8
        rcopies.append(
            pltpu.make_async_remote_copy(
                src_ref=sendb.at[jj], dst_ref=recvb.at[dj],
                send_sem=rsend.at[dj], recv_sem=rrecv.at[dj],
                device_id=device(m, jj),
            )
        )
    for c in rcopies:
        c.start()
    for c in rcopies:
        c.wait_recv()
    g_own, q_own = j // 4, j % 4
    for k in range(16):
        total = turn[g_own, k, pl.ds(pl.multiple_of(q_own * 8, 8), 8), :]
        for dj in range(1, 8):
            total = total + recvb[dj, :, 128 * k : 128 * k + 128].astype(F32)
        out[:, 128 * k : 128 * k + 128] = total
    for c in jcopies + mcopies + rcopies:
        c.wait_send()


def body(sinogram, jitter, shift):
    vmem = pl.BlockSpec(memory_space=pltpu.VMEM)
    image = pl.pallas_call(
        kernel,
        out_shape=jax.ShapeDtypeStruct((8, BINS), F32),
        in_specs=[vmem] * 3,
        out_specs=vmem,
        scratch_shapes=[
            pltpu.VMEM((STRIP, 128), BF16),
            pltpu.VMEM((64, 256), F32),
            pltpu.VMEM((8, 8, BINS), BF16),
            pltpu.VMEM((24, 1, 128), F32),
            pltpu.VMEM((8 * TILES * 8, 128), F32),
            pltpu.VMEM((8 * TILES * 8, 128), F32),
            pltpu.VMEM((4, 8, 128), F32),
            pltpu.VMEM((8, 128), jnp.int32),
            pltpu.SMEM((4, 8, 128), F32),
            pltpu.SMEM((8, 128), jnp.int32),
            pltpu.VMEM((2, 16, 4, 8, 128), F32),
            pltpu.VMEM((2, 16, 32, 128), F32),
            pltpu.VMEM((8, 8, BINS), BF16),
            pltpu.VMEM((8, 8, BINS), BF16),
            pltpu.SemaphoreType.DMA((24,)),
            pltpu.SemaphoreType.DMA((24,)),
            pltpu.SemaphoreType.DMA((8,)),
            pltpu.SemaphoreType.DMA((8,)),
            pltpu.SemaphoreType.DMA((8,)),
            pltpu.SemaphoreType.DMA((8,)),
            pltpu.SemaphoreType.DMA((2,)),
        ],
        compiler_params=pltpu.CompilerParams(collective_id=0, has_side_effects=True),
    )(sinogram, jitter.reshape(1, 2), shift.reshape(1, 128))
    return image.reshape(2, 4, BINS)


def solution(mesh):
    return jax.shard_map(
        body,
        mesh=mesh,
        in_specs=(P("blk", "slab", None), P("blk"), P()),
        out_specs=P("blk", "slab", None),
        check_vma=False,
    )
```

time: 695 us -> 32.9 us (0.05)
  the two profiles are of different devices: /device:TPU:0 before, /device:TPU:1 now
where the time goes in v1:
time: 32.9 us; the launch traced here: 32.7 us
  Pallas kernels  31.2 us (95%)
  local copies, waits for them, and re-layouts  1.49 us (5%)
    pallas_call x1, Pallas kernels, body(): pl.pallas_call(kernel, out_shape=jax.ShapeDtypeStruct((8, BINS), F32), in...  31.2 us
    reshape x1, local copies, waits for them, and re-layouts, body(): return image.reshape(2, 4, BINS)  1.49 us

profile of v1, /device:TPU:1, one launch (start us, length us, event | category | flops | bytes accessed | tf_op | source)
XLA Modules:
  0.0 32.7 jit_solution(13405972909301367143)
XLA Ops:
  0.0 31.2 %shard_map.37 = f32[8,2048]{1,0:T(8,128)} custom-call(bf16[2,4,2048]{2,1,0:T(4,128)(2,1)} %sino.1, bf16[1,2]{1,0:T(2,128)(2,1)} %bitcast.2, s32[1,128]{1,0:T(1,128)} %bitcast.3), custom_call_target="tpu_custom_call" | custom-call | tf_op jit(solution)/shard_map/pallas_call | solution.py:275
  31.2 1.5 %reshape.11 = f32[2,4,2048]{2,1,0:T(4,128)} reshape(f32[8,2048]{1,0:T(8,128)} %shard_map.37) | data formatting | bytes 131072 | tf_op jit(solution)/shard_map/reshape | solution.py:305

commit v2 on v1

v2 whole, which is shorter than its diff:
```python
import functools
import math

import jax
import jax.numpy as jnp
from jax import lax
from jax.experimental import pallas as pl
from jax.experimental.pallas import tpu as pltpu
from jax.sharding import PartitionSpec as P

BINS = 2048
ANGLES = 128
NROWS = 128
TILES = 18
STRIP = 3968
ROWS = 8 * TILES * 16
F32 = jnp.float32
BF16 = jnp.bfloat16


def hop(r):
    dz = jnp.where((r == 0) | (r == 1) | (r == 2) | (r == 6), 0, 1)
    dx = jnp.where(
        (r == 0) | (r == 3), 0, jnp.where((r == 1) | (r == 4), 1, jnp.where((r == 2) | (r == 5), 3, 2))
    )
    return dz, dx


def source_of(m, r):
    dz, dx = hop(r)
    return ((m // 4 + dz) % 2) * 4 + (m % 4 + 4 - dx) % 4


def target_of(m, r):
    dz, dx = hop(r)
    return ((m // 4 + dz) % 2) * 4 + (m % 4 + dx) % 4


def lane_gather(x, idx):
    dims = lax.GatherDimensionNumbers(
        offset_dims=(),
        collapsed_slice_dims=(1,),
        start_index_map=(1,),
        operand_batching_dims=(0,),
        start_indices_batching_dims=(0,),
    )
    return lax.gather(
        x, idx[:, :, None], dims, slice_sizes=(1, 1), mode=lax.GatherScatterMode.PROMISE_IN_BOUNDS
    )


def build_strip(strip):
    shape = (128, 128)
    diff = lax.broadcasted_iota(jnp.int32, shape, 1) - lax.broadcasted_iota(jnp.int32, shape, 0)
    odd = (diff % 2) != 0
    diff_f = diff.astype(F32)

    def chunk(c, _):
        n = diff_f + (1920 - 128 * c).astype(F32)
        value = jnp.where(odd, (-1.0 / math.pi**2) / (n * n), 0.0)
        value = jnp.where(n == 0.0, 0.25, value)
        strip[pl.ds(pl.multiple_of(c * 128, 128), 128), :] = value.astype(BF16)
        return 0

    lax.fori_loop(0, STRIP // 128, chunk, 0)


def filter_rows(sino, strip, flat, msg):
    x = jnp.concatenate([sino[0].astype(F32), sino[1].astype(F32)], axis=0)
    xs = jnp.concatenate([x[:, 256 * i : 256 * i + 256] for i in range(8)], axis=0).astype(BF16)
    for d in range(-7, 8):
        rhs = jnp.concatenate(
            [strip[1920 - 128 * e : 1920 - 128 * e + 256, :] for e in (2 * d, 2 * d + 1)], axis=1
        )
        part = jnp.dot(xs, rhs, preferred_element_type=F32)
        for i in range(max(0, -d), min(8, 8 - d)):
            j = i + d
            piece = part[8 * i : 8 * i + 8, :]
            if i == 7:
                flat[8 * j : 8 * j + 8, :] = piece
            else:
                flat[8 * j : 8 * j + 8, :] += piece
    for j in range(8):
        msg[0, :, 256 * j : 256 * j + 256] = flat[8 * j : 8 * j + 8, :].astype(BF16)


def kernel(
    sino, jit, shift, out,
    strip, flat, msg, jr, taps, tsrc, isrc, stab, itab, acc, turn, sendb, recvb,
    jsend, jrecv, tsend, trecv, isend, irecv, msend, mrecv, rsend, rrecv,
):
    idx = lax.axis_index("blk")
    m = idx // 8
    j = idx % 8
    barrier = pltpu.get_barrier_semaphore()
    shape = (8, 128)
    lane = lax.broadcasted_iota(jnp.int32, shape, 1)
    sub = lax.broadcasted_iota(jnp.int32, shape, 0)
    lane_f = lane.astype(F32)
    sub_f = sub.astype(F32)
    zero = jnp.zeros(shape, F32)

    def device(mm, jj):
        return {"blk": mm * 8 + jj}

    for dj in (-1, 0, 1):
        for r in range(8):
            if dj == 0 and r == 0:
                continue
            pl.semaphore_signal(barrier, inc=1, device_id=device(target_of(m, r), (j + dj + 8) % 8))
    for dj in (2, 3, 4, 5, 6):
        pl.semaphore_signal(barrier, inc=1, device_id=device(m, (j + dj) % 8))

    jv = jit[...].astype(F32)
    jr[8] = jnp.concatenate([jnp.broadcast_to(jv[:, a : a + 1], (1, 128)) for a in range(2)], axis=0)

    a_l = (lane // 32) % 2
    g_l = (lane // 16) % 2
    k_l = lane % 16
    own_jit = jnp.where(a_l == 0, jnp.broadcast_to(jv[:, 0:1], shape), jnp.broadcast_to(jv[:, 1:2], shape))
    angle = m * 16 + 2 * j + a_l
    theta = (angle.astype(F32) + own_jit) * math.pi / ANGLES
    cosine = jnp.cos(theta)
    sine = jnp.sin(theta)
    offset = lane_gather(jnp.broadcast_to(shift[...], shape), angle).astype(F32)
    center = (
        cosine * (128.0 * k_l.astype(F32) - (BINS - 1) / 2)
        + sine * ((16 * target_of(m, sub) + 8 * g_l).astype(F32) - (NROWS - 1) / 2)
        + ((BINS - 1) / 2 + 128.0 + offset)
    )
    lowest = center + jnp.minimum(0.0, 127.0 * cosine) + jnp.minimum(0.0, 7.0 * sine) - 0.01
    tile_f = jnp.clip(jnp.floor(lowest * (1.0 / 128.0)), 0.0, TILES - 2.0)
    base_f = center - 128.0 * tile_f
    first_row = (sub * TILES + tile_f.astype(jnp.int32)) * 16 + 4 * a_l
    for r in range(8):
        tsrc[r] = jnp.concatenate([x[r : r + 1, :] for x in (base_f, cosine, sine, sine)], axis=0)
        isrc[r] = first_row[r : r + 1, :]
    own_tables = [
        pltpu.make_async_copy(tsrc.at[0], stab.at[0], tsend.at[0]),
        pltpu.make_async_copy(isrc.at[0], itab.at[0], isend.at[0]),
    ]
    for c in own_tables:
        c.start()

    build_strip(strip)
    filter_rows(sino, strip, flat, msg)
    acc[...] = jnp.zeros_like(acc)
    for c in own_tables:
        c.wait()

    pl.semaphore_wait(barrier, 28)

    jcopies = []
    tcopies = []
    mcopies = []
    for dj in (0, -1, 1):
        jj = (j - dj + 8) % 8
        base = m if dj == 0 else (jnp.where(j == 0, (m + 7) % 8, m) if dj == 1 else jnp.where(j == 7, (m + 1) % 8, m))
        for r in range(8):
            if dj == 0 and r == 0:
                continue
            slot = (dj + 1) * 8 + r
            jcopies.append(
                pltpu.make_async_remote_copy(
                    src_ref=jr.at[8], dst_ref=jr.at[slot],
                    send_sem=jsend.at[slot], recv_sem=jrecv.at[slot],
                    device_id=device(target_of(base, r), jj),
                )
            )
    for r in range(1, 8):
        tcopies.append(
            pltpu.make_async_remote_copy(
                src_ref=tsrc.at[r], dst_ref=stab.at[r],
                send_sem=tsend.at[r], recv_sem=trecv.at[r],
                device_id=device(target_of(m, r), j),
            )
        )
        tcopies.append(
            pltpu.make_async_remote_copy(
                src_ref=isrc.at[r], dst_ref=itab.at[r],
                send_sem=isend.at[r], recv_sem=irecv.at[r],
                device_id=device(target_of(m, r), j),
            )
        )
        mcopies.append(
            pltpu.make_async_remote_copy(
                src_ref=msg.at[0], dst_ref=msg.at[r],
                send_sem=msend.at[r], recv_sem=mrecv.at[r],
                device_id=device(target_of(m, r), j),
            )
        )
    for c in jcopies + tcopies + mcopies:
        c.start()
    for c in jcopies:
        c.wait_recv()

    last = lane == 127
    lane_1 = lane_f + 1.0

    def arrive(r):
        @pl.when(r > 0)
        def _():
            pltpu.make_async_copy(msg.at[0], msg.at[0], mrecv.at[r]).wait()
            pltpu.make_async_copy(stab.at[0], stab.at[0], trecv.at[r]).wait()
            pltpu.make_async_copy(itab.at[0], itab.at[0], irecv.at[r]).wait()

    def expand(r):
        own, before, after = jr[8 + r], jr[r], jr[16 + r]
        scale = 4.0 / math.sqrt(ANGLES)
        w0 = (1.0 + (own[1:2, :] - before[1:2, :]) * 1.5) * scale
        w1 = (1.0 + (after[0:1, :] - own[0:1, :]) * 1.5) * scale
        w = jnp.where(sub < 4, jnp.broadcast_to(w0, shape), jnp.broadcast_to(w1, shape))
        base = r * (TILES * 16)

        def put(t, value):
            taps[pl.ds(pl.multiple_of(base + t * 8, 8), 8), :] = value

        prev, prev_rolled = zero, zero
        put(0, zero)
        for t in range(1, TILES):
            if t < TILES - 1:
                f = msg[r, :, 128 * (t - 1) : 128 * t].astype(F32) * w
                rolled = pltpu.roll(f, 127, 1)
            else:
                f, rolled = zero, zero
            put(2 * t, f)
            put(2 * t - 1, jnp.where(last, rolled, prev_rolled) - prev)
            prev, prev_rolled = f, rolled
        put(2 * TILES - 1, zero)

    def ramps_of(r):
        out_r = []
        for a in range(2):
            cos_a, sin_a = stab[r, 1, 32 * a], stab[r, 2, 32 * a]
            step = cos_a * (1.0 - 2e-6)
            rise = sin_a * sub_f
            edge = jnp.where(cos_a >= 0.0, 0.0, 127.0)
            out_r.append((step * lane_f + rise, step * jnp.broadcast_to(edge, shape) + rise))
        return out_r

    def block(r, g, ramps):
        for k in range(16):
            total = [acc[g, k, s] for s in range(4)]
            for a in range(2):
                col = 32 * a + 16 * g + k
                start = stab[r, 0, col]
                row = jnp.clip(itab[r, 0, col], 0, ROWS - 28)
                v = ramps[a][0] + start
                cell = v.astype(jnp.int32)
                frac = v - cell.astype(F32)
                upper = ramps[a][1] + start >= lane_1
                pick = cell & 127
                for s in range(4):
                    def at(o):
                        low = jnp.broadcast_to(taps[pl.ds(row + o, 1), :], shape)
                        high = jnp.broadcast_to(taps[pl.ds(row + (o + 16), 1), :], shape)
                        return lane_gather(jnp.where(upper, high, low), pick)

                    total[s] = total[s] + (at(s) + frac * at(s + 8))
            for s in range(4):
                acc[g, k, s] = total[s]

    g_own, q_own = j // 4, j % 4
    g_far = 1 - g_own
    rcopies = []

    def finish(g, qs):
        for k in range(16):
            for s in range(4):
                turn[g, k, pl.ds(s, 8, stride=4), :] = acc[g, k, s]
        for q in range(4):
            for k in range(16):
                sendb[4 * g + q, :, 128 * k : 128 * k + 128] = turn[g, k, 8 * q : 8 * q + 8, :].astype(BF16)
        for q in qs:
            jj = 4 * g + q
            dj = (jj - j + 8) % 8
            c = pltpu.make_async_remote_copy(
                src_ref=sendb.at[jj], dst_ref=recvb.at[dj],
                send_sem=rsend.at[dj], recv_sem=rrecv.at[dj],
                device_id=device(m, jj),
            )
            c.start()
            rcopies.append(c)

    def early(r, _):
        arrive(r)
        expand(r)
        ramps = ramps_of(r)
        for g in range(2):
            block(r, g, ramps)
        return 0

    lax.fori_loop(0, 4, early, 0)

    def unpack(r, _):
        arrive(r)
        expand(r)
        return 0

    lax.fori_loop(4, 8, unpack, 0)

    def late(g):
        def step(i, _):
            for r in (4 + 2 * i, 5 + 2 * i):
                block(r, g, ramps_of(r))
            return 0

        lax.fori_loop(0, 2, step, 0)

    late(g_far)
    finish(g_far, range(4))
    late(g_own)
    finish(g_own, [(q_own + i) % 4 for i in (1, 2, 3)])

    for dj in range(1, 8):
        pltpu.make_async_copy(recvb.at[0], recvb.at[0], rrecv.at[dj]).wait()
    for k in range(16):
        total = turn[g_own, k, pl.ds(pl.multiple_of(q_own * 8, 8), 8), :]
        for dj in range(1, 8):
            total = total + recvb[dj, :, 128 * k : 128 * k + 128].astype(F32)
        out[:, 128 * k : 128 * k + 128] = total
    for c in jcopies + tcopies + mcopies + rcopies:
        c.wait_send()


def body(sinogram, jitter, shift):
    vmem = pl.BlockSpec(memory_space=pltpu.VMEM)
    image = pl.pallas_call(
        kernel,
        out_shape=jax.ShapeDtypeStruct((8, BINS), F32),
        in_specs=[vmem] * 3,
        out_specs=vmem,
        scratch_shapes=[
            pltpu.VMEM((STRIP, 128), BF16),
            pltpu.VMEM((64, 256), F32),
            pltpu.VMEM((8, 8, BINS), BF16),
            pltpu.VMEM((24, 2, 128), F32),
            pltpu.VMEM((ROWS, 128), F32),
            pltpu.VMEM((8, 4, 128), F32),
            pltpu.VMEM((8, 1, 128), jnp.int32),
            pltpu.SMEM((8, 4, 128), F32),
            pltpu.SMEM((8, 1, 128), jnp.int32),
            pltpu.VMEM((2, 16, 4, 8, 128), F32),
            pltpu.VMEM((2, 16, 32, 128), F32),
            pltpu.VMEM((8, 8, BINS), BF16),
            pltpu.VMEM((8, 8, BINS), BF16),
            pltpu.SemaphoreType.DMA((24,)),
            pltpu.SemaphoreType.DMA((24,)),
            pltpu.SemaphoreType.DMA((8,)),
            pltpu.SemaphoreType.DMA((8,)),
            pltpu.SemaphoreType.DMA((8,)),
            pltpu.SemaphoreType.DMA((8,)),
            pltpu.SemaphoreType.DMA((8,)),
            pltpu.SemaphoreType.DMA((8,)),
            pltpu.SemaphoreType.DMA((8,)),
            pltpu.SemaphoreType.DMA((8,)),
        ],
        compiler_params=pltpu.CompilerParams(collective_id=0, has_side_effects=True),
    )(sinogram, jitter.reshape(1, 2), shift.reshape(1, 128))
    return image.reshape(2, 4, BINS)


def solution(mesh):
    return jax.shard_map(
        body,
        mesh=mesh,
        in_specs=(P("blk", "slab", None), P("blk"), P()),
        out_specs=P("blk", "slab", None),
        check_vma=False,
    )
```

time: 32.9 us -> 26 us (0.79)
  Pallas kernels: 31.2 us -> 24.3 us
    pallas_call x1, Pallas kernels: 31.2 us -> 24.3 us  [body(): pl.pallas_call(kernel, out_shape=jax.ShapeDtypeStruct((8, BINS), F32), in...]
where the time goes in v2:
time: 26 us; the launch traced here: 25.8 us
  Pallas kernels  24.3 us (93%)
  local copies, waits for them, and re-layouts  1.49 us (6%)
    pallas_call x1, Pallas kernels, body(): pl.pallas_call(kernel, out_shape=jax.ShapeDtypeStruct((8, BINS), F32), in...  24.3 us
    reshape x1, local copies, waits for them, and re-layouts, body(): return image.reshape(2, 4, BINS)  1.49 us

profile of v2, /device:TPU:1, one launch (start us, length us, event | category | flops | bytes accessed | tf_op | source)
XLA Modules:
  0.0 25.8 jit_solution(16201981705582603474)
XLA Ops:
  0.0 24.3 %shard_map.37 = f32[8,2048]{1,0:T(8,128)} custom-call(bf16[2,4,2048]{2,1,0:T(4,128)(2,1)} %sino.1, bf16[1,2]{1,0:T(2,128)(2,1)} %bitcast.2, s32[1,128]{1,0:T(1,128)} %bitcast.3), custom_call_target="tpu_custom_call" | custom-call | tf_op jit(solution)/shard_map/pallas_call | solution.py:328
  24.3 1.5 %reshape.11 = f32[2,4,2048]{2,1,0:T(4,128)} reshape(f32[8,2048]{1,0:T(8,128)} %shard_map.37) | data formatting | bytes 131072 | tf_op jit(solution)/shard_map/reshape | solution.py:360

commit v3 on v2

--- a/solution.py
+++ b/solution.py
@@ -13,7 +13,10 @@
 NROWS = 128
 TILES = 18
 STRIP = 3968
-ROWS = 8 * TILES * 16
+ROWS = 8 * TILES * 8
+WIDE = BINS + 128
+FULL = 16383.0
+TINY = 1e-30
 F32 = jnp.float32
 BF16 = jnp.bfloat16
 
@@ -80,13 +83,20 @@
                 flat[8 * j : 8 * j + 8, :] = piece
             else:
                 flat[8 * j : 8 * j + 8, :] += piece
+    peak = jnp.zeros((8, 128), F32)
     for j in range(8):
-        msg[0, :, 256 * j : 256 * j + 256] = flat[8 * j : 8 * j + 8, :].astype(BF16)
+        rows = flat[8 * j : 8 * j + 8, :].astype(BF16)
+        msg[0, :, 256 * j : 256 * j + 256] = rows
+        size = jnp.abs(rows.astype(F32))
+        peak = jnp.maximum(peak, jnp.maximum(size[:, :128], size[:, 128:]))
+    peak = jnp.broadcast_to(jnp.max(peak, axis=1, keepdims=True), (8, 128))
+    peak = jnp.maximum(peak, jnp.concatenate([peak[4:8], peak[0:4]], axis=0))
+    msg[0, :, BINS:WIDE] = peak.astype(BF16)
 
 
 def kernel(
     sino, jit, shift, out,
-    strip, flat, msg, jr, taps, tsrc, isrc, stab, itab, acc, turn, sendb, recvb,
+    strip, flat, msg, jr, taps, unit, alone, tsrc, isrc, stab, itab, acc, turn, sendb, recvb,
     jsend, jrecv, tsend, trecv, isend, irecv, msend, mrecv, rsend, rrecv,
 ):
     idx = lax.axis_index("blk")
@@ -131,7 +141,7 @@
     lowest = center + jnp.minimum(0.0, 127.0 * cosine) + jnp.minimum(0.0, 7.0 * sine) - 0.01
     tile_f = jnp.clip(jnp.floor(lowest * (1.0 / 128.0)), 0.0, TILES - 2.0)
     base_f = center - 128.0 * tile_f
-    first_row = (sub * TILES + tile_f.astype(jnp.int32)) * 16 + 4 * a_l
+    first_row = (sub * TILES + tile_f.astype(jnp.int32)) * 8 + 4 * a_l
     for r in range(8):
         tsrc[r] = jnp.concatenate([x[r : r + 1, :] for x in (base_f, cosine, sine, sine)], axis=0)
         isrc[r] = first_row[r : r + 1, :]
@@ -144,7 +154,6 @@
 
     build_strip(strip)
     filter_rows(sino, strip, flat, msg)
-    acc[...] = jnp.zeros_like(acc)
     for c in own_tables:
         c.wait()
 
@@ -191,42 +200,49 @@
         )
     for c in jcopies + tcopies + mcopies:
         c.start()
-    for c in jcopies:
-        c.wait_recv()
 
     last = lane == 127
     lane_1 = lane_f + 1.0
 
-    def arrive(r):
-        @pl.when(r > 0)
-        def _():
-            pltpu.make_async_copy(msg.at[0], msg.at[0], mrecv.at[r]).wait()
-            pltpu.make_async_copy(stab.at[0], stab.at[0], trecv.at[r]).wait()
-            pltpu.make_async_copy(itab.at[0], itab.at[0], irecv.at[r]).wait()
-
-    def expand(r):
+    def weights_of(r):
         own, before, after = jr[8 + r], jr[r], jr[16 + r]
         scale = 4.0 / math.sqrt(ANGLES)
         w0 = (1.0 + (own[1:2, :] - before[1:2, :]) * 1.5) * scale
         w1 = (1.0 + (after[0:1, :] - own[0:1, :]) * 1.5) * scale
-        w = jnp.where(sub < 4, jnp.broadcast_to(w0, shape), jnp.broadcast_to(w1, shape))
-        base = r * (TILES * 16)
-
-        def put(t, value):
-            taps[pl.ds(pl.multiple_of(base + t * 8, 8), 8), :] = value
+        return jnp.broadcast_to(w0, shape), jnp.broadcast_to(w1, shape)
+
+    def jitter_from(r, classes):
+        for dj in classes:
+            pltpu.make_async_copy(jr.at[0], jr.at[0], jrecv.at[(dj + 1) * 8 + r]).wait()
+
+    def arrive(r):
+        jitter_from(r, (0, -1, 1))
+        pltpu.make_async_copy(stab.at[0], stab.at[0], trecv.at[r]).wait()
+        pltpu.make_async_copy(itab.at[0], itab.at[0], irecv.at[r]).wait()
+        pltpu.make_async_copy(msg.at[0], msg.at[0], mrecv.at[r]).wait()
+
+    def expand(r, w0, w1):
+        top = jnp.maximum(w0, w1)
+        peak = msg[r, :, BINS:WIDE].astype(F32)
+        unit[r] = peak * top * (1.0 / (FULL * 65536.0))
+        gain = jnp.where(sub < 4, w0, w1) * FULL / (top * jnp.maximum(peak, TINY))
+        base = r * (TILES * 8)
+
+        def put(t, value, after):
+            whole = jnp.round(value).astype(jnp.int32)
+            half = jnp.round((after - value) * 0.5).astype(jnp.int32)
+            taps[pl.ds(pl.multiple_of(base + t * 8, 8), 8), :] = whole * 65536 + half
 
         prev, prev_rolled = zero, zero
-        put(0, zero)
         for t in range(1, TILES):
             if t < TILES - 1:
-                f = msg[r, :, 128 * (t - 1) : 128 * t].astype(F32) * w
+                f = msg[r, :, 128 * (t - 1) : 128 * t].astype(F32) * gain
                 rolled = pltpu.roll(f, 127, 1)
             else:
                 f, rolled = zero, zero
-            put(2 * t, f)
-            put(2 * t - 1, jnp.where(last, rolled, prev_rolled) - prev)
+            put(t - 1, prev, jnp.where(last, rolled, prev_rolled))
             prev, prev_rolled = f, rolled
-        put(2 * TILES - 1, zero)
+        taps[pl.ds(pl.multiple_of(base + (TILES - 1) * 8, 8), 8), :] = jnp.zeros(shape, jnp.int32)
 
     def ramps_of(r):
         out_r = []
@@ -238,27 +254,37 @@
             out_r.append((step * lane_f + rise, step * jnp.broadcast_to(edge, shape) + rise))
         return out_r
 
+    def picked(r, g, k, a, ramp):
+        col = 32 * a + 16 * g + k
+        start = stab[r, 0, col]
+        row = jnp.clip(itab[r, 0, col], 0, ROWS - 12)
+        v = ramp[0] + start
+        cell = v.astype(jnp.int32)
+        frac = v - cell.astype(F32)
+        upper = ramp[1] + start >= lane_1
+        pick = cell & 127
+        words = []
+        for s in range(4):
+            low = jnp.broadcast_to(taps[pl.ds(row + s, 1), :], shape)
+            high = jnp.broadcast_to(taps[pl.ds(row + (s + 8), 1), :], shape)
+            words.append(lane_gather(jnp.where(upper, high, low), pick))
+        return words, 2.0 * frac - 1.0 / 65536.0
+
     def block(r, g, ramps):
         for k in range(16):
-            total = [acc[g, k, s] for s in range(4)]
+            (x0, t0), (x1, t1) = [picked(r, g, k, a, ramps[a]) for a in range(2)]
+            for s in range(4):
+                both = (x0[s] + x1[s]).astype(F32)
+                both = both + (x0[s] * 65536).astype(F32) * t0 + (x1[s] * 65536).astype(F32) * t1
+                scale = jnp.broadcast_to(unit[r, s : s + 1, :], shape)
+                acc[g, k, s] = acc[g, k, s] + scale * both
+
+    def first_block(g, ramps):
+        for k in range(16):
             for a in range(2):
-                col = 32 * a + 16 * g + k
-                start = stab[r, 0, col]
-                row = jnp.clip(itab[r, 0, col], 0, ROWS - 28)
-                v = ramps[a][0] + start
-                cell = v.astype(jnp.int32)
-                frac = v - cell.astype(F32)
-                upper = ramps[a][1] + start >= lane_1
-                pick = cell & 127
+                x, t = picked(0, g, k, a, ramps[a])
                 for s in range(4):
-                    def at(o):
-                        low = jnp.broadcast_to(taps[pl.ds(row + o, 1), :], shape)
-                        high = jnp.broadcast_to(taps[pl.ds(row + (o + 16), 1), :], shape)
-                        return lane_gather(jnp.where(upper, high, low), pick)
-
-                    total[s] = total[s] + (at(s) + frac * at(s + 8))
-            for s in range(4):
-                acc[g, k, s] = total[s]
+                    alone[a, g, k, s] = x[s].astype(F32) + (x[s] * 65536).astype(F32) * t
 
     g_own, q_own = j // 4, j % 4
     g_far = 1 - g_own
@@ -282,19 +308,36 @@
             c.start()
             rcopies.append(c)
 
+    one = jnp.ones(shape, F32)
+    expand(0, one, one)
+    ramps = ramps_of(0)
+
+    def own_angles(g, _):
+        first_block(g, ramps)
+        return 0
+
+    lax.fori_loop(0, 2, own_angles, 0)
+    jitter_from(0, (-1, 1))
+    w0, w1 = weights_of(0)
+    for g in range(2):
+        for k in range(16):
+            for s in range(4):
+                scale = jnp.broadcast_to(unit[0, s : s + 1, :], shape)
+                acc[g, k, s] = scale * (w0 * alone[0, g, k, s] + w1 * alone[1, g, k, s])
+
     def early(r, _):
         arrive(r)
-        expand(r)
+        expand(r, *weights_of(r))
         ramps = ramps_of(r)
         for g in range(2):
             block(r, g, ramps)
         return 0
 
-    lax.fori_loop(0, 4, early, 0)
+    lax.fori_loop(1, 4, early, 0)
 
     def unpack(r, _):
         arrive(r)
-        expand(r)
+        expand(r, *weights_of(r))
         return 0
 
     lax.fori_loop(4, 8, unpack, 0)
@@ -333,9 +376,11 @@
         scratch_shapes=[
             pltpu.VMEM((STRIP, 128), BF16),
             pltpu.VMEM((64, 256), F32),
-            pltpu.VMEM((8, 8, BINS), BF16),
+            pltpu.VMEM((8, 8, WIDE), BF16),
             pltpu.VMEM((24, 2, 128), F32),
-            pltpu.VMEM((ROWS, 128), F32),
+            pltpu.VMEM((ROWS, 128), jnp.int32),
+            pltpu.VMEM((8, 8, 128), F32),
+            pltpu.VMEM((2, 2, 16, 4, 8, 128), F32),
             pltpu.VMEM((8, 4, 128), F32),
             pltpu.VMEM((8, 1, 128), jnp.int32),
             pltpu.SMEM((8, 4, 128), F32),

time: 26 us -> 23.8 us (0.915)
  Pallas kernels: 24.3 us -> 22.1 us
    pallas_call x1, Pallas kernels: 24.3 us -> 22.1 us  [body(): pl.pallas_call(kernel, out_shape=jax.ShapeDtypeStruct((8, BINS), F32), in...]
where the time goes in v3:
time: 23.8 us; the launch traced here: 23.6 us
  Pallas kernels  22.1 us (93%)
  local copies, waits for them, and re-layouts  1.49 us (6%)
    pallas_call x1, Pallas kernels, body(): pl.pallas_call(kernel, out_shape=jax.ShapeDtypeStruct((8, BINS), F32), in...  22.1 us
    reshape x1, local copies, waits for them, and re-layouts, body(): return image.reshape(2, 4, BINS)  1.49 us

profile of v3, /device:TPU:1, one launch (start us, length us, event | category | flops | bytes accessed | tf_op | source)
XLA Modules:
  0.0 23.6 jit_solution(14902387659185304378)
XLA Ops:
  0.0 22.1 %shard_map.37 = f32[8,2048]{1,0:T(8,128)} custom-call(bf16[2,4,2048]{2,1,0:T(4,128)(2,1)} %sino.1, bf16[1,2]{1,0:T(2,128)(2,1)} %bitcast.2, s32[1,128]{1,0:T(1,128)} %bitcast.3), custom_call_target="tpu_custom_call" | custom-call | tf_op jit(solution)/shard_map/pallas_call | solution.py:371
  22.1 1.5 %reshape.11 = f32[2,4,2048]{2,1,0:T(4,128)} reshape(f32[8,2048]{1,0:T(8,128)} %shard_map.37) | data formatting | bytes 131072 | tf_op jit(solution)/shard_map/reshape | solution.py:405

commit v4 on v3

--- a/solution.py
+++ b/solution.py
@@ -231,7 +231,7 @@
         def put(t, value, after):
             whole = jnp.round(value).astype(jnp.int32)
             half = jnp.round((after - value) * 0.5).astype(jnp.int32)
-            taps[pl.ds(pl.multiple_of(base + t * 8, 8), 8), :] = whole * 65536 + half
+            taps[pl.ds(pl.multiple_of(base + t * 8, 8), 8), :] = lax.shift_left(whole, 16) + half
 
         prev, prev_rolled = zero, zero
         for t in range(1, TILES):
@@ -275,7 +275,7 @@
             (x0, t0), (x1, t1) = [picked(r, g, k, a, ramps[a]) for a in range(2)]
             for s in range(4):
                 both = (x0[s] + x1[s]).astype(F32)
-                both = both + (x0[s] * 65536).astype(F32) * t0 + (x1[s] * 65536).astype(F32) * t1
+                both = both + lax.shift_left(x0[s], 16).astype(F32) * t0 + lax.shift_left(x1[s], 16).astype(F32) * t1
                 scale = jnp.broadcast_to(unit[r, s : s + 1, :], shape)
                 acc[g, k, s] = acc[g, k, s] + scale * both
 
@@ -284,7 +284,7 @@
             for a in range(2):
                 x, t = picked(0, g, k, a, ramps[a])
                 for s in range(4):
-                    alone[a, g, k, s] = x[s].astype(F32) + (x[s] * 65536).astype(F32) * t
+                    alone[a, g, k, s] = x[s].astype(F32) + lax.shift_left(x[s], 16).astype(F32) * t
 
     g_own, q_own = j // 4, j % 4
     g_far = 1 - g_own
@@ -294,11 +294,11 @@
         for k in range(16):
             for s in range(4):
                 turn[g, k, pl.ds(s, 8, stride=4), :] = acc[g, k, s]
-        for q in range(4):
-            for k in range(16):
-                sendb[4 * g + q, :, 128 * k : 128 * k + 128] = turn[g, k, 8 * q : 8 * q + 8, :].astype(BF16)
         for q in qs:
             jj = 4 * g + q
+            for k in range(16):
+                rows = turn[g, k, pl.ds(pl.multiple_of(8 * q, 8), 8), :]
+                sendb[jj, :, 128 * k : 128 * k + 128] = rows.astype(BF16)
             dj = (jj - j + 8) % 8
             c = pltpu.make_async_remote_copy(
                 src_ref=sendb.at[jj], dst_ref=recvb.at[dj],
@@ -351,9 +351,10 @@
         lax.fori_loop(0, 2, step, 0)
 
     late(g_far)
-    finish(g_far, range(4))
+    y_odd = (j // 2) % 2
+    finish(g_far, [(2 * y_odd + i) % 4 for i in range(4)])
     late(g_own)
-    finish(g_own, [(q_own + i) % 4 for i in (1, 2, 3)])
+    finish(g_own, [2 - 2 * y_odd, 3 - 2 * y_odd, 2 * y_odd + (1 - j % 2)])
 
     for dj in range(1, 8):
         pltpu.make_async_copy(recvb.at[0], recvb.at[0], rrecv.at[dj]).wait()
@@ -400,7 +401,7 @@
             pltpu.SemaphoreType.DMA((8,)),
             pltpu.SemaphoreType.DMA((8,)),
         ],
-        compiler_params=pltpu.CompilerParams(collective_id=0, has_side_effects=True),
+        compiler_params=pltpu.CompilerParams(collective_id=0, has_side_effects=True, vmem_limit_bytes=16 * 1024 * 1024),
     )(sinogram, jitter.reshape(1, 2), shift.reshape(1, 128))
     return image.reshape(2, 4, BINS)
 

time: 23.8 us -> 23 us (0.966)
  Pallas kernels: 22.1 us -> 20.8 us
  local copies, waits for them, and re-layouts: 1.49 us -> 2.08 us
    unnamed x0 -> x6, local copies, waits for them, and re-layouts: none -> 1.43 us
    pallas_call x1, Pallas kernels: 22.1 us -> 20.8 us  [body(): pl.pallas_call(kernel, out_shape=jax.ShapeDtypeStruct((8, BINS), F32), in...]
    reshape x1, local copies, waits for them, and re-layouts: 1.49 us -> 0.65 us  [body(): return image.reshape(2, 4, BINS)]
where the time goes in v4:
time: 23 us; the launch traced here: 22.8 us
  Pallas kernels  20.8 us (90%)
  local copies, waits for them, and re-layouts  2.08 us (9%)
    pallas_call x1, Pallas kernels, body(): pl.pallas_call(kernel, out_shape=jax.ShapeDtypeStruct((8, BINS), F32), in...  20.8 us
    unnamed x6, local copies, waits for them, and re-layouts  1.43 us
    reshape x1, local copies, waits for them, and re-layouts, body(): return image.reshape(2, 4, BINS)  0.65 us

profile of v4, /device:TPU:1, one launch (start us, length us, event | category | flops | bytes accessed | tf_op | source)
XLA Modules:
  0.0 22.8 jit_solution(447793380211988168)
XLA Ops:
  0.0 0.0 copy-start.1
  0.0 0.0 copy-start.2
  0.0 0.7 %copy-done.1 = bf16[2]{0:T(256)(128)(2,1)S(1)} copy-done((bf16[2]{0:T(256)(128)(2,1)S(1)}, bf16[2]{0:T(256)(128)(2,1)}, u32[]{:S(2)}) %copy-start.1) | copy-done | bytes 28
  0.7 0.0 copy-done.2
  0.7 0.0 copy-start
  0.7 0.8 %copy-done = bf16[2,4,2048]{2,1,0:T(4,128)(2,1)S(1)} copy-done((bf16[2,4,2048]{2,1,0:T(4,128)(2,1)S(1)}, bf16[2,4,2048]{2,1,0:T(4,128)(2,1)}, u32[]{:S(2)}) %copy-start) | copy-done | bytes 32792
  1.4 20.8 %shard_map.37 = f32[8,2048]{1,0:T(8,128)S(1)} custom-call(bf16[2,4,2048]{2,1,0:T(4,128)(2,1)S(1)} %copy-done, bf16[1,2]{1,0:T(2,128)(2,1)S(1)} %bitcast.2, s32[1,128]{1,0:T(1,128)S(1)} %bitcast.3), custom_call_target="tpu_custom_call" | custom-call | tf_op jit(solution)/shard_map/pallas_call | solution.py:372
  22.2 0.7 %reshape.11 = f32[2,4,2048]{2,1,0:T(4,128)} reshape(f32[8,2048]{1,0:T(8,128)S(1)} %shard_map.37) | data formatting | bytes 131072 | tf_op jit(solution)/shard_map/reshape | solution.py:406
Async XLA Ops:
  0.0 0.7 %copy-start.1 = (bf16[2]{0:T(256)(128)(2,1)S(1)}, bf16[2]{0:T(256)(128)(2,1)}, u32[]{:S(2)}) copy-start(bf16[2]{0:T(256)(128)(2,1)} %param.4) | copy-start | bytes 16
  0.0 0.7 %copy-start.2 = (s32[128]{0:T(128)S(1)}, s32[128]{0:T(128)}, u32[]{:S(2)}) copy-start(s32[128]{0:T(128)} %param.5) | copy-start | bytes 1540
  0.7 0.8 %copy-start = (bf16[2,4,2048]{2,1,0:T(4,128)(2,1)S(1)}, bf16[2,4,2048]{2,1,0:T(4,128)(2,1)}, u32[]{:S(2)}) copy-start(bf16[2,4,2048]{2,1,0:T(4,128)(2,1)} %sino.1) | copy-start | bytes 98308

commit v5 on v4

--- a/solution.py
+++ b/solution.py
@@ -270,14 +270,19 @@
             words.append(lane_gather(jnp.where(upper, high, low), pick))
         return words, 2.0 * frac - 1.0 / 65536.0
 
+    def source_terms(r, g, k, ramps):
+        (x0, t0), (x1, t1) = [picked(r, g, k, a, ramps[a]) for a in range(2)]
+        terms = []
+        for s in range(4):
+            both = (x0[s] + x1[s]).astype(F32)
+            both = both + lax.shift_left(x0[s], 16).astype(F32) * t0 + lax.shift_left(x1[s], 16).astype(F32) * t1
+            terms.append(jnp.broadcast_to(unit[r, s : s + 1, :], shape) * both)
+        return terms
+
     def block(r, g, ramps):
         for k in range(16):
-            (x0, t0), (x1, t1) = [picked(r, g, k, a, ramps[a]) for a in range(2)]
-            for s in range(4):
-                both = (x0[s] + x1[s]).astype(F32)
-                both = both + lax.shift_left(x0[s], 16).astype(F32) * t0 + lax.shift_left(x1[s], 16).astype(F32) * t1
-                scale = jnp.broadcast_to(unit[r, s : s + 1, :], shape)
-                acc[g, k, s] = acc[g, k, s] + scale * both
+            for s, term in enumerate(source_terms(r, g, k, ramps)):
+                acc[g, k, s] = acc[g, k, s] + term
 
     def first_block(g, ramps):
         for k in range(16):
@@ -290,19 +295,25 @@
     g_far = 1 - g_own
     rcopies = []
 
-    def finish(g, qs):
-        for k in range(16):
+    def late(g, half, qs):
+        ramps = [ramps_of(r) for r in range(4, 8)]
+        for k in range(8 * half, 8 * half + 8):
+            total = [acc[g, k, s] for s in range(4)]
+            for r in range(4, 8):
+                scaled = source_terms(r, g, k, ramps[r - 4])
+                total = [t + c for t, c in zip(total, scaled)]
             for s in range(4):
-                turn[g, k, pl.ds(s, 8, stride=4), :] = acc[g, k, s]
+                turn[g, k, pl.ds(s, 8, stride=4), :] = total[s]
+        columns = pl.ds(1024 * half, 1024)
         for q in qs:
             jj = 4 * g + q
-            for k in range(16):
+            for k in range(8 * half, 8 * half + 8):
                 rows = turn[g, k, pl.ds(pl.multiple_of(8 * q, 8), 8), :]
                 sendb[jj, :, 128 * k : 128 * k + 128] = rows.astype(BF16)
             dj = (jj - j + 8) % 8
             c = pltpu.make_async_remote_copy(
-                src_ref=sendb.at[jj], dst_ref=recvb.at[dj],
-                send_sem=rsend.at[dj], recv_sem=rrecv.at[dj],
+                src_ref=sendb.at[jj, :, columns], dst_ref=recvb.at[dj, :, columns],
+                send_sem=rsend.at[half, dj], recv_sem=rrecv.at[half, dj],
                 device_id=device(m, jj),
             )
             c.start()
@@ -342,23 +353,17 @@
 
     lax.fori_loop(4, 8, unpack, 0)
 
-    def late(g):
-        def step(i, _):
-            for r in (4 + 2 * i, 5 + 2 * i):
-                block(r, g, ramps_of(r))
-            return 0
-
-        lax.fori_loop(0, 2, step, 0)
-
-    late(g_far)
     y_odd = (j // 2) % 2
-    finish(g_far, [(2 * y_odd + i) % 4 for i in range(4)])
-    late(g_own)
-    finish(g_own, [2 - 2 * y_odd, 3 - 2 * y_odd, 2 * y_odd + (1 - j % 2)])
-
-    for dj in range(1, 8):
-        pltpu.make_async_copy(recvb.at[0], recvb.at[0], rrecv.at[dj]).wait()
+    for half in range(2):
+        late(g_far, half, [(2 * y_odd + i) % 4 for i in range(4)])
+    for half in range(2):
+        late(g_own, half, [2 - 2 * y_odd, 3 - 2 * y_odd, 2 * y_odd + (1 - j % 2)])
+
+    half_row = recvb.at[0, :, pl.ds(0, 1024)]
     for k in range(16):
+        if k % 8 == 0:
+            for dj in range(1, 8):
+                pltpu.make_async_copy(half_row, half_row, rrecv.at[k // 8, dj]).wait()
         total = turn[g_own, k, pl.ds(pl.multiple_of(q_own * 8, 8), 8), :]
         for dj in range(1, 8):
             total = total + recvb[dj, :, 128 * k : 128 * k + 128].astype(F32)
@@ -398,8 +403,8 @@
             pltpu.SemaphoreType.DMA((8,)),
             pltpu.SemaphoreType.DMA((8,)),
             pltpu.SemaphoreType.DMA((8,)),
-            pltpu.SemaphoreType.DMA((8,)),
-            pltpu.SemaphoreType.DMA((8,)),
+            pltpu.SemaphoreType.DMA((2, 8)),
+            pltpu.SemaphoreType.DMA((2, 8)),
         ],
         compiler_params=pltpu.CompilerParams(collective_id=0, has_side_effects=True, vmem_limit_bytes=16 * 1024 * 1024),
     )(sinogram, jitter.reshape(1, 2), shift.reshape(1, 128))

time: 23 us -> 22.6 us (0.983)
  Pallas kernels: 20.8 us -> 20.3 us
    pallas_call x1, Pallas kernels: 20.8 us -> 20.3 us  [body(): pl.pallas_call(kernel, out_shape=jax.ShapeDtypeStruct((8, BINS), F32), in...]
where the time goes in v5:
time: 22.6 us; the launch traced here: 22.4 us
  Pallas kernels  20.3 us (90%)
  local copies, waits for them, and re-layouts  2.08 us (9%)
    pallas_call x1, Pallas kernels, body(): pl.pallas_call(kernel, out_shape=jax.ShapeDtypeStruct((8, BINS), F32), in...  20.3 us
    unnamed x6, local copies, waits for them, and re-layouts  1.43 us
    reshape x1, local copies, waits for them, and re-layouts, body(): return image.reshape(2, 4, BINS)  0.65 us

profile of v5, /device:TPU:1, one launch (start us, length us, event | category | flops | bytes accessed | tf_op | source)
XLA Modules:
  0.0 22.4 jit_solution(74633919111150600)
XLA Ops:
  0.0 0.0 copy-start.1
  0.0 0.0 copy-start.2
  0.0 0.7 %copy-done.1 = bf16[2]{0:T(256)(128)(2,1)S(1)} copy-done((bf16[2]{0:T(256)(128)(2,1)S(1)}, bf16[2]{0:T(256)(128)(2,1)}, u32[]{:S(2)}) %copy-start.1) | copy-done | bytes 28
  0.7 0.0 copy-done.2
  0.7 0.0 copy-start
  0.7 0.8 %copy-done = bf16[2,4,2048]{2,1,0:T(4,128)(2,1)S(1)} copy-done((bf16[2,4,2048]{2,1,0:T(4,128)(2,1)S(1)}, bf16[2,4,2048]{2,1,0:T(4,128)(2,1)}, u32[]{:S(2)}) %copy-start) | copy-done | bytes 32792
  1.4 20.3 %shard_map.37 = f32[8,2048]{1,0:T(8,128)S(1)} custom-call(bf16[2,4,2048]{2,1,0:T(4,128)(2,1)S(1)} %copy-done, bf16[1,2]{1,0:T(2,128)(2,1)S(1)} %bitcast.2, s32[1,128]{1,0:T(1,128)S(1)} %bitcast.3), custom_call_target="tpu_custom_call" | custom-call | tf_op jit(solution)/shard_map/pallas_call | solution.py:377
  21.8 0.7 %reshape.11 = f32[2,4,2048]{2,1,0:T(4,128)} reshape(f32[8,2048]{1,0:T(8,128)S(1)} %shard_map.37) | data formatting | bytes 131072 | tf_op jit(solution)/shard_map/reshape | solution.py:411
Async XLA Ops:
  0.0 0.7 %copy-start.1 = (bf16[2]{0:T(256)(128)(2,1)S(1)}, bf16[2]{0:T(256)(128)(2,1)}, u32[]{:S(2)}) copy-start(bf16[2]{0:T(256)(128)(2,1)} %param.4) | copy-start | bytes 16
  0.0 0.7 %copy-start.2 = (s32[128]{0:T(128)S(1)}, s32[128]{0:T(128)}, u32[]{:S(2)}) copy-start(s32[128]{0:T(128)} %param.5) | copy-start | bytes 1540
  0.7 0.8 %copy-start = (bf16[2,4,2048]{2,1,0:T(4,128)(2,1)S(1)}, bf16[2,4,2048]{2,1,0:T(4,128)(2,1)}, u32[]{:S(2)}) copy-start(bf16[2,4,2048]{2,1,0:T(4,128)(2,1)} %sino.1) | copy-start | bytes 98308

commit v6 on v5

--- a/solution.py
+++ b/solution.py
@@ -346,12 +346,10 @@
 
     lax.fori_loop(1, 4, early, 0)
 
-    def unpack(r, _):
+    for r in range(4, 8):
         arrive(r)
+    for r in range(4, 8):
         expand(r, *weights_of(r))
-        return 0
-
-    lax.fori_loop(4, 8, unpack, 0)
 
     y_odd = (j // 2) % 2
     for half in range(2):

time: 22.6 us -> 22.4 us (level)
    pallas_call x1, Pallas kernels: 20.3 us -> 20.1 us  [body(): pl.pallas_call(kernel, out_shape=jax.ShapeDtypeStruct((8, BINS), F32), in...]
where the time goes in v6:
time: 22.4 us; the launch traced here: 22.2 us
  Pallas kernels  20.1 us (90%)
  local copies, waits for them, and re-layouts  2.08 us (9%)
    pallas_call x1, Pallas kernels, body(): pl.pallas_call(kernel, out_shape=jax.ShapeDtypeStruct((8, BINS), F32), in...  20.1 us
    unnamed x6, local copies, waits for them, and re-layouts  1.43 us
    reshape x1, local copies, waits for them, and re-layouts, body(): return image.reshape(2, 4, BINS)  0.65 us

profile of v6, /device:TPU:1, one launch (start us, length us, event | category | flops | bytes accessed | tf_op | source)
XLA Modules:
  0.0 22.2 jit_solution(7354399183837086938)
XLA Ops:
  0.0 0.0 copy-start.1
  0.0 0.0 copy-start.2
  0.0 0.7 %copy-done.1 = bf16[2]{0:T(256)(128)(2,1)S(1)} copy-done((bf16[2]{0:T(256)(128)(2,1)S(1)}, bf16[2]{0:T(256)(128)(2,1)}, u32[]{:S(2)}) %copy-start.1) | copy-done | bytes 28
  0.7 0.0 copy-done.2
  0.7 0.0 copy-start
  0.7 0.8 %copy-done = bf16[2,4,2048]{2,1,0:T(4,128)(2,1)S(1)} copy-done((bf16[2,4,2048]{2,1,0:T(4,128)(2,1)S(1)}, bf16[2,4,2048]{2,1,0:T(4,128)(2,1)}, u32[]{:S(2)}) %copy-start) | copy-done | bytes 32792
  1.4 20.1 %shard_map.37 = f32[8,2048]{1,0:T(8,128)S(1)} custom-call(bf16[2,4,2048]{2,1,0:T(4,128)(2,1)S(1)} %copy-done, bf16[1,2]{1,0:T(2,128)(2,1)S(1)} %bitcast.2, s32[1,128]{1,0:T(1,128)S(1)} %bitcast.3), custom_call_target="tpu_custom_call" | custom-call | tf_op jit(solution)/shard_map/pallas_call | solution.py:375
  21.5 0.7 %reshape.11 = f32[2,4,2048]{2,1,0:T(4,128)} reshape(f32[8,2048]{1,0:T(8,128)S(1)} %shard_map.37) | data formatting | bytes 131072 | tf_op jit(solution)/shard_map/reshape | solution.py:409
Async XLA Ops:
  0.0 0.7 %copy-start.1 = (bf16[2]{0:T(256)(128)(2,1)S(1)}, bf16[2]{0:T(256)(128)(2,1)}, u32[]{:S(2)}) copy-start(bf16[2]{0:T(256)(128)(2,1)} %param.4) | copy-start | bytes 16
  0.0 0.7 %copy-start.2 = (s32[128]{0:T(128)S(1)}, s32[128]{0:T(128)}, u32[]{:S(2)}) copy-start(s32[128]{0:T(128)} %param.5) | copy-start | bytes 1540
  0.7 0.8 %copy-start = (bf16[2,4,2048]{2,1,0:T(4,128)(2,1)S(1)}, bf16[2,4,2048]{2,1,0:T(4,128)(2,1)}, u32[]{:S(2)}) copy-start(bf16[2,4,2048]{2,1,0:T(4,128)(2,1)} %sino.1) | copy-start | bytes 98308

commit v7 on v6

--- a/solution.py
+++ b/solution.py
@@ -344,7 +344,22 @@
             block(r, g, ramps)
         return 0
 
-    lax.fori_loop(1, 4, early, 0)
+    early(1, 0)
+    for r in (2, 3):
+        arrive(r)
+    for r in (2, 3):
+        expand(r, *weights_of(r))
+    pair_ramps = [ramps_of(r) for r in (2, 3)]
+
+    def pair(g, _):
+        for k in range(16):
+            first = source_terms(2, g, k, pair_ramps[0])
+            second = source_terms(3, g, k, pair_ramps[1])
+            for s in range(4):
+                acc[g, k, s] = acc[g, k, s] + (first[s] + second[s])
+        return 0
+
+    lax.fori_loop(0, 2, pair, 0)
 
     for r in range(4, 8):
         arrive(r)

time: 22.4 us -> 22.3 us (level)
  no operation moved by 1% of the time
where the time goes in v7:
time: 22.3 us; the launch traced here: 22.1 us
  Pallas kernels  20 us (90%)
  local copies, waits for them, and re-layouts  2.08 us (9%)
    pallas_call x1, Pallas kernels, body(): pl.pallas_call(kernel, out_shape=jax.ShapeDtypeStruct((8, BINS), F32), in...  20 us
    unnamed x6, local copies, waits for them, and re-layouts  1.43 us
    reshape x1, local copies, waits for them, and re-layouts, body(): return image.reshape(2, 4, BINS)  0.65 us

profile of v7, /device:TPU:1, one launch (start us, length us, event | category | flops | bytes accessed | tf_op | source)
XLA Modules:
  0.0 22.1 jit_solution(10610234096601252020)
XLA Ops:
  0.0 0.0 copy-start.1
  0.0 0.0 copy-start.2
  0.0 0.7 %copy-done.1 = bf16[2]{0:T(256)(128)(2,1)S(1)} copy-done((bf16[2]{0:T(256)(128)(2,1)S(1)}, bf16[2]{0:T(256)(128)(2,1)}, u32[]{:S(2)}) %copy-start.1) | copy-done | bytes 28
  0.7 0.0 copy-done.2
  0.7 0.0 copy-start
  0.7 0.8 %copy-done = bf16[2,4,2048]{2,1,0:T(4,128)(2,1)S(1)} copy-done((bf16[2,4,2048]{2,1,0:T(4,128)(2,1)S(1)}, bf16[2,4,2048]{2,1,0:T(4,128)(2,1)}, u32[]{:S(2)}) %copy-start) | copy-done | bytes 32792
  1.4 20.0 %shard_map.37 = f32[8,2048]{1,0:T(8,128)S(1)} custom-call(bf16[2,4,2048]{2,1,0:T(4,128)(2,1)S(1)} %copy-done, bf16[1,2]{1,0:T(2,128)(2,1)S(1)} %bitcast.2, s32[1,128]{1,0:T(1,128)S(1)} %bitcast.3), custom_call_target="tpu_custom_call" | custom-call | tf_op jit(solution)/shard_map/pallas_call | solution.py:390
  21.5 0.7 %reshape.11 = f32[2,4,2048]{2,1,0:T(4,128)} reshape(f32[8,2048]{1,0:T(8,128)S(1)} %shard_map.37) | data formatting | bytes 131072 | tf_op jit(solution)/shard_map/reshape | solution.py:424
Async XLA Ops:
  0.0 0.7 %copy-start.1 = (bf16[2]{0:T(256)(128)(2,1)S(1)}, bf16[2]{0:T(256)(128)(2,1)}, u32[]{:S(2)}) copy-start(bf16[2]{0:T(256)(128)(2,1)} %param.4) | copy-start | bytes 16
  0.0 0.7 %copy-start.2 = (s32[128]{0:T(128)S(1)}, s32[128]{0:T(128)}, u32[]{:S(2)}) copy-start(s32[128]{0:T(128)} %param.5) | copy-start | bytes 1540
  0.7 0.8 %copy-start = (bf16[2,4,2048]{2,1,0:T(4,128)(2,1)S(1)}, bf16[2,4,2048]{2,1,0:T(4,128)(2,1)}, u32[]{:S(2)}) copy-start(bf16[2,4,2048]{2,1,0:T(4,128)(2,1)} %sino.1) | copy-start | bytes 98308
